TPU v7x, 32 devices: a whole 2x2x4 slice. The times are simulated.
32 devices in a mesh: ga: 8 (over y, x, core), ka: 4 (over z).
Axes of the slice: x: 2, y: 2, z: 4, core: 2. Of those that a mesh axis runs over, the one named last changes fastest.
Arguments:
- fine_waves: bfloat16 [64, 16, 40960], P('ka', None, 'ga'), may hold values from -6 to 6
- coarse_waves: bfloat16 [32, 16, 40960], P('ka', None, 'ga'), may hold values from -6 to 6
- coarse_kernel: bfloat16 [48, 64, 2048], P('ga', None, 'ka'), may hold values from -6 to 6
- row_valence: float32 [8, 8, 8, 8], P('ga'), may hold values from -6 to 6
- row_conduction: float32 [8, 8, 8, 8], P('ga'), may hold values from -6 to 6
- row_neighbours: int32 [8, 8], P('ga'), may hold values from 0 to 11, as said below
- row_weight_index: int32 [8, 8], P('ga'), may hold values from 0 to 7
- col_neighbours: int32 [64, 8], P('ka'), may hold values from 0 to 7, as said below
- col_weight_index: int32 [64, 8], P('ka'), may hold values from 0 to 7
- tile_list: int32 [4, 8], replicated, may hold values from 0 to 31, as said below
- weight_table: float32 [8], replicated, may hold values from 0.2 to 0.5
Outputs:
- fine_kernel: bfloat16 [8, 64, 4096], P('ga', 'ka')
Inputs may be any that keep to these rules, and one draw needn't show every extreme that they name: `row_neighbours`: each row names 8 distinct positions; a position p below 6 is coarse row p of the fine row's own group r, a larger one is coarse row p - 6 of the next group (the last group's next is group 0); each row names three or more of each kind. `col_neighbours`: each fine column names 8 distinct positions of its owner's list, and every position of the list is named by some column of that owner. `tile_list`: row o lists 8 distinct coarse columns in rising order of their holder (column p is held by owner p // 8); no row takes more than 4 columns from one holder, and every row takes exactly 4 from some holder.
All inputs are finite; a program needn't handle non-finite values.
Results may differ from a plain program's by a relative error of at most 0.0064.
Values may be sent and summed in bfloat16 or wider, within the bound.
No kernel may reach another device: no remote copies, remote signals or barrier semaphores. Data moves between devices by JAX's collectives and lax.ppermute only.
A program may use at most 64 MiB of HBM per device.

v0:
```python
import functools
import itertools
import math

import jax
import jax.numpy as jnp
import numpy as np
from jax import lax
from jax.experimental import pallas as pl
from jax.experimental.pallas import tpu as pltpu
from jax.sharding import PartitionSpec as P


VALENCE = 8
CONDUCTION = 8
BANDS = VALENCE + CONDUCTION
PLANE_WAVES = 40960
CORNERS = 8
BAND_PAIRS = 64
SLOT_COUNT = 4
HALF = SLOT_COUNT // 2
FAR = (2, 3)


VMEM = pl.BlockSpec(memory_space=pltpu.VMEM)
SMEM = pl.BlockSpec(memory_space=pltpu.SMEM)
ANY = pl.BlockSpec(memory_space=pl.ANY)
LIMIT = pltpu.CompilerParams(vmem_limit_bytes=16 * 2**20)


def passed_along(array, axis, by):
    peers = lax.axis_size(axis)
    return lax.ppermute(array, axis, [(i, (i + by) % peers) for i in range(peers)])


def swapped(array, axis, mask):
    peers = lax.axis_size(axis)
    return lax.ppermute(array, axis, [(i, i ^ mask) for i in range(peers)])


def slots_for(list_ref, owner, me, held, slots):
    length = list_ref.shape[1]

    def step(place, carry):
        rank, ids = carry[0], carry[1:]
        column = list_ref[owner, place]
        mine = lax.div(column, held) == me
        ids = tuple(
            jnp.where(jnp.logical_and(mine, rank == slot), column - me * held, ids[slot])
            for slot in range(slots)
        )
        return (rank + jnp.where(mine, 1, 0),) + ids

    zero = jnp.int32(0)
    return lax.fori_loop(0, length, step, (zero,) * (slots + 1), unroll=length <= 8)[1:]


def later_index(list_ref, held):
    wants, which, crowded = [], [], jnp.int32(0)
    for owner in range(4):
        count = []
        for mask in FAR:
            total = jnp.int32(0)
            for place in range(list_ref.shape[1]):
                holder = lax.div(list_ref[owner, place], held)
                total = total + jnp.where(holder == owner ^ mask, 1, 0)
            count.append(total > HALF)
        wants.append(jnp.where(jnp.logical_or(*count), 1, 0))
        which.append(jnp.where(count[0], 0, jnp.where(count[1], 1, 0)))
        crowded = crowded + jnp.where(jnp.logical_and(*count), 1, 0)
    level = jnp.maximum(wants[0] + wants[1], wants[2] + wants[3])
    codes = []
    for half in (0, 2):
        one = jnp.where(
            wants[half] > 0, which[half], jnp.where(wants[half + 1] > 0, 2 + which[half + 1], 0)
        )
        codes.append(jnp.where(level == 2, which[half] * 2 + which[half + 1], one))
    index = jnp.where(level == 0, 0, 16 * level - 15 + codes[0] * 4 + codes[1])
    return jnp.where(crowded > 0, 33, index)


def later_options():
    def single(half, code):
        return [(2 * half + code // 2, code % 2)]

    def double(half, code):
        return [(2 * half, code // 2), (2 * half + 1, code % 2)]

    options = [[]]
    for chosen in (single, double):
        for low, high in itertools.product(range(4), repeat=2):
            options.append(chosen(0, low) + chosen(1, high))
    return options + [list(itertools.product(range(4), range(2)))]


def pack_kernel(blocks, me_ref, list_ref, waves_ref, *rest):
    outs, index_ref, sems = rest[:-2], rest[-2], rest[-1]
    held = waves_ref.shape[0]
    me = me_ref[0]
    copies = []
    slots = {}
    for (mask, low, high), out in zip(blocks, outs):
        if mask not in slots:
            slots[mask] = slots_for(
                list_ref, lax.bitwise_xor(me, mask), me, held, SLOT_COUNT
            )
        for slot in range(low, high):
            copy = pltpu.make_async_copy(
                waves_ref.at[slots[mask][slot]], out.at[slot - low], sems.at[len(copies)]
            )
            copy.start()
            copies.append(copy)
    index_ref[0] = later_index(list_ref, held) if list_ref.shape[0] == 4 else jnp.int32(0)
    for copy in copies:
        copy.wait()


def packed_waves(me, tile_list, coarse_waves, blocks):
    _, bands, waves = coarse_waves.shape
    shapes = [
        jax.ShapeDtypeStruct((high - low, bands, waves), coarse_waves.dtype)
        for _, low, high in blocks
    ]
    copies = sum(high - low for _, low, high in blocks)
    return pl.pallas_call(
        functools.partial(pack_kernel, blocks),
        out_shape=shapes + [jax.ShapeDtypeStruct((1,), jnp.int32)],
        in_specs=[SMEM, SMEM, VMEM],
        out_specs=[ANY] * len(blocks) + [SMEM],
        scratch_shapes=[pltpu.SemaphoreType.DMA((copies,))],
        name="pack",
    )(me, tile_list, coarse_waves)


def wave_blocks(peers):
    masks = sorted(range(1, peers), reverse=True)
    if peers != 4:
        return [(mask, 0, SLOT_COUNT) for mask in masks], []
    always = [(mask, 0, HALF) for mask in FAR] + [(1, 0, SLOT_COUNT)]
    return always, [(mask, HALF, SLOT_COUNT) for mask in FAR]


def sent_where_needed(index, packed):
    def sending(option, *packed):
        sent = []
        for which, mask in enumerate(FAR):
            pairs = [(o ^ mask, o) for o, at in option if at == which]
            sent.append(lax.ppermute(packed[which], "ka", pairs) if pairs else packed[which])
        return tuple(sent)

    branches = [functools.partial(sending, option) for option in later_options()]
    return lax.switch(index, branches, *packed)


def split_dot(left, right):
    high = left.astype(jnp.bfloat16)
    rest = left - high.astype(jnp.float32)
    middle = rest.astype(jnp.bfloat16)
    low = (rest - middle.astype(jnp.float32)).astype(jnp.bfloat16)
    parts = [jnp.dot(x, right, preferred_element_type=jnp.float32) for x in (high, middle, low)]
    return (parts[0] + parts[1]) + parts[2]


def turned(small):
    count = small.shape[1]
    rows = lax.broadcasted_iota(jnp.int32, (count, count), 0)
    columns = lax.broadcasted_iota(jnp.int32, (count, count), 1)
    unit = (rows == columns).astype(jnp.float32).astype(jnp.bfloat16)
    values = small.astype(jnp.float32).astype(jnp.bfloat16)
    return lax.dot_general(
        unit, values, (((1,), (1,)), ((), ())), preferred_element_type=jnp.float32
    ).astype(jnp.int32)


def rotate_kernel(
    peers,
    me_ref,
    list_ref,
    near_ref,
    level_ref,
    table_ref,
    valence_ref,
    conduction_ref,
    neighbours_ref,
    levels_ref,
    own_ref,
    next_ref,
    *rest,
):
    outs, scale_ref, (chosen, wide, mats) = rest[:peers], rest[peers], rest[peers + 1 :]
    group = own_ref.shape[0]
    held = own_ref.shape[2] // BAND_PAIRS
    me = me_ref[0]
    for corner in range(CORNERS):
        place = near_ref[0, corner]
        rows = pl.ds(corner * BAND_PAIRS, BAND_PAIRS)

        @pl.when(place < group)
        def _():
            chosen[rows, :] = own_ref[place]

        @pl.when(place >= group)
        def _():
            chosen[rows, :] = next_ref[place - group]

    lanes = lax.broadcasted_iota(jnp.int32, (VALENCE, BAND_PAIRS), 1)
    bands = lax.broadcasted_iota(jnp.int32, (VALENCE, BAND_PAIRS), 0)
    by_valence = (lanes // CONDUCTION == bands).astype(jnp.float32).astype(jnp.bfloat16)
    by_conduction = (lanes % CONDUCTION == bands).astype(jnp.float32).astype(jnp.bfloat16)
    rows = CORNERS * VALENCE
    wide[...] = split_dot(valence_ref[0].reshape(rows, VALENCE), by_valence)
    conduction = split_dot(conduction_ref[0].reshape(rows, CONDUCTION), by_conduction)
    norm = 1.0 / math.sqrt(BAND_PAIRS)
    for corner in range(0, CORNERS, 2):
        for v in range(VALENCE):
            pair = []
            for c in (corner, corner + 1):
                outer_product = (
                    wide[pl.ds(c * VALENCE + v, 1), :]
                    * conduction[c * CONDUCTION : (c + 1) * CONDUCTION]
                )
                pair.append(table_ref[level_ref[0, c]] * outer_product * norm)
            mats[
                pl.ds(v * CONDUCTION, CONDUCTION),
                corner * BAND_PAIRS : (corner + 2) * BAND_PAIRS,
            ] = jnp.concatenate(pair, axis=1)

    product = jnp.dot(
        mats[...].astype(jnp.bfloat16), chosen[...], preferred_element_type=jnp.float32
    )
    product = product.astype(jnp.bfloat16)
    tiles = [product[:, p * BAND_PAIRS : (p + 1) * BAND_PAIRS] for p in range(held)]
    for mask in range(peers):
        ids = slots_for(list_ref, lax.bitwise_xor(me, mask), me, held, SLOT_COUNT)
        picked = []
        for slot in range(SLOT_COUNT):
            tile = tiles[0]
            for p in range(1, held):
                tile = jnp.where(ids[slot] == p, tiles[p], tile)
            picked.append(tile)
        outs[mask][...] = jnp.concatenate(picked, axis=1)

    fine_count = neighbours_ref.shape[1]
    width = scale_ref.shape[1]
    neighbours, levels = turned(neighbours_ref[...]), turned(levels_ref[...])
    weights = jnp.zeros(levels.shape, jnp.float32)
    for level in range(table_ref.shape[0]):
        weights = jnp.where(levels == level, table_ref[level], weights)
    lane = lax.broadcasted_iota(jnp.int32, (fine_count, width), 1)
    weight = jnp.zeros((fine_count, width), jnp.float32)
    for corner in range(CORNERS):
        named = neighbours[:, corner : corner + 1] == lane // BANDS
        weight = weight + jnp.where(named, weights[:, corner : corner + 1], 0.0)
    inv_root = 1.0 / math.sqrt(PLANE_WAVES)
    factor = jnp.where(lane % BANDS < VALENCE, inv_root, weight * (inv_root * norm))
    for fine in range(fine_count):
        scale_ref[pl.ds(fine * VALENCE, VALENCE), :] = jnp.broadcast_to(
            factor[fine : fine + 1], (VALENCE, width)
        )


def rotated_tiles(me, tile_list, row_args, col_args, weight_table, own, upper):
    peers, length = tile_list.shape
    near, level, valence, conduction = row_args
    columns = own.shape[2]
    block = jax.ShapeDtypeStruct((BAND_PAIRS, SLOT_COUNT * BAND_PAIRS), jnp.bfloat16)
    scale = jax.ShapeDtypeStruct((col_args[0].shape[1] * VALENCE, length * BANDS), jnp.float32)
    return pl.pallas_call(
        functools.partial(rotate_kernel, peers),
        out_shape=[block] * peers + [scale],
        in_specs=[SMEM] * 5 + [VMEM] * 6,
        out_specs=[VMEM] * (peers + 1),
        scratch_shapes=[
            pltpu.VMEM((CORNERS * BAND_PAIRS, columns), jnp.bfloat16),
            pltpu.VMEM((CORNERS * VALENCE, BAND_PAIRS), jnp.float32),
            pltpu.VMEM((BAND_PAIRS, CORNERS * BAND_PAIRS), jnp.float32),
        ],
        name="rotate",
    )(me, tile_list, near, level, weight_table, valence, conduction, *col_args, own, upper)


def list_places(list_ref, me, held):
    entries = []
    rank, last = jnp.int32(0), jnp.int32(-1)
    for place in range(list_ref.shape[1]):
        column = list_ref[me, place]
        holder = lax.div(column, held)
        rank = jnp.where(holder == last, rank + 1, 0)
        last = holder
        entries.append((column, lax.bitwise_xor(holder, me), rank))
    return entries


def correlate_kernel(blocks, me_ref, list_ref, fine_hbm, own_ref, *rest):
    arrived, (out_ref, fine, listed, sems) = rest[: len(blocks)], rest[len(blocks) :]
    held = own_ref.shape[0]
    me = me_ref[0]
    fine_count, bands, waves = fine_hbm.shape
    length = listed.shape[0]
    parts = sems.shape[0]
    count = fine_count // parts
    copies = []
    for part in range(parts):
        some = pl.ds(part * count, count)
        copies.append(pltpu.make_async_copy(fine_hbm.at[some], fine.at[some], sems.at[part]))
        copies[-1].start()
    for place, (column, mask, rank) in enumerate(list_places(list_ref, me, held)):

        def fetch(source, at, place=place):
            listed[place] = source[at]

        pl.when(mask == 0)(functools.partial(fetch, own_ref, column - me * held))
        for (other, low, high), source in zip(blocks, arrived):
            here = jnp.logical_and(rank >= low, rank < high)
            pl.when(jnp.logical_and(mask == other, here))(
                functools.partial(fetch, source, rank - low)
            )
    for part in range(parts):
        copies[part].wait()
        dense = lax.dot_general(
            fine[part * count : (part + 1) * count].reshape(count * bands, waves),
            listed[...].reshape(length * bands, waves),
            (((1,), (1,)), ((), ())),
            preferred_element_type=jnp.float32,
        )
        dense = dense.reshape(count, 2, VALENCE, length * bands)
        lanes = lax.broadcasted_iota(jnp.int32, (count, VALENCE, length * bands), 2)
        both = jnp.where(lanes % bands < VALENCE, dense[:, 0], dense[:, 1])
        out_ref[pl.ds(part * count * VALENCE, count * VALENCE), :] = both.reshape(
            count * VALENCE, length * bands
        )


def partial_correlations(me, tile_list, fine_waves, coarse_waves, blocks, arrived):
    fine_count, bands, waves = fine_waves.shape
    length = tile_list.shape[1]
    return pl.pallas_call(
        functools.partial(correlate_kernel, blocks),
        out_shape=jax.ShapeDtypeStruct((fine_count * VALENCE, length * bands), jnp.float32),
        in_specs=[SMEM, SMEM, ANY] + [VMEM] * (1 + len(blocks)),
        out_specs=VMEM,
        scratch_shapes=[
            pltpu.VMEM((fine_count, bands, waves), jnp.bfloat16),
            pltpu.VMEM((length, bands, waves), jnp.bfloat16),
            pltpu.SemaphoreType.DMA((2 if fine_count % 2 == 0 else 1,)),
        ],
        compiler_params=LIMIT,
        name="correlate",
    )(
        me,
        tile_list,
        pltpu.with_memory_space_constraint(fine_waves, pltpu.HBM),
        coarse_waves,
        *arrived,
    )


def finish_kernel(peers, held, me_ref, list_ref, parts_ref, scale_ref, spread_ref, *rest):
    tiles_in, (out_ref, tiles, left, wide, rotation, blocks) = rest[:peers], rest[peers:]
    me = me_ref[0]
    fine_count = out_ref.shape[0]
    length = list_ref.shape[1]
    width = length * BAND_PAIRS
    for mask in range(peers):
        tiles[mask] = tiles_in[mask][...]
    for place, (column, mask, rank) in enumerate(list_places(list_ref, me, held)):
        block = tiles[mask]
        tile = block[:, :BAND_PAIRS]
        for slot in range(1, SLOT_COUNT):
            tile = jnp.where(
                rank == slot, block[:, slot * BAND_PAIRS : (slot + 1) * BAND_PAIRS], tile
            )
        left[:, place * BAND_PAIRS : (place + 1) * BAND_PAIRS] = tile

    total = jnp.sum(parts_ref[...], axis=0) * scale_ref[...]
    wide[...] = split_dot(total, spread_ref[...])

    for fine in range(fine_count):
        conduction = wide[pl.ds(fine * CONDUCTION, CONDUCTION), width:]
        for v in range(0, VALENCE, 2):
            pair = [
                wide[pl.ds(fine * VALENCE + v + i, 1), :width] * conduction for i in range(2)
            ]
            rotation[pl.ds((fine * VALENCE + v) * CONDUCTION, 2 * CONDUCTION), :] = (
                jnp.concatenate(pair, axis=0).astype(jnp.bfloat16)
            )
    for fine in range(fine_count):
        blocks[pl.ds(fine * BAND_PAIRS, BAND_PAIRS), :] = lax.dot_general(
            left[...],
            rotation[pl.ds(fine * BAND_PAIRS, BAND_PAIRS), :],
            (((1,), (1,)), ((), ())),
            preferred_element_type=jnp.float32,
        )
    for pair in range(0, BAND_PAIRS, 2):
        rows = [blocks[pl.ds(pair + i, fine_count, stride=BAND_PAIRS), :] for i in range(2)]
        out_ref[:, pair * BAND_PAIRS : (pair + 2) * BAND_PAIRS] = jnp.concatenate(
            rows, axis=1
        ).astype(jnp.bfloat16)


def spread_matrix(length):
    rows = np.arange(length * BANDS)[:, None]
    lanes = np.arange(length * BAND_PAIRS)[None, :]
    place, w, y = lanes // BAND_PAIRS, lanes // CONDUCTION % VALENCE, lanes % CONDUCTION
    valence = rows == place * BANDS + w
    conduction = rows == place * BANDS + VALENCE + y
    return jnp.asarray(np.concatenate([valence, conduction], axis=1), dtype=jnp.bfloat16)


def finished(me, tile_list, parts, scale, tiles, held, fine_count):
    length = tile_list.shape[1]
    peers = len(tiles)
    return pl.pallas_call(
        functools.partial(finish_kernel, peers, held),
        out_shape=jax.ShapeDtypeStruct((fine_count, BAND_PAIRS * BAND_PAIRS), jnp.bfloat16),
        in_specs=[SMEM, SMEM] + [VMEM] * (3 + peers),
        out_specs=VMEM,
        scratch_shapes=[
            pltpu.VMEM((peers, BAND_PAIRS, SLOT_COUNT * BAND_PAIRS), jnp.bfloat16),
            pltpu.VMEM((BAND_PAIRS, length * BAND_PAIRS), jnp.bfloat16),
            pltpu.VMEM((fine_count * VALENCE, 2 * length * BAND_PAIRS), jnp.float32),
            pltpu.VMEM((fine_count * BAND_PAIRS, length * BAND_PAIRS), jnp.bfloat16),
            pltpu.VMEM((fine_count * BAND_PAIRS, BAND_PAIRS), jnp.float32),
        ],
        compiler_params=LIMIT,
        name="finish",
    )(me, tile_list, parts, scale, spread_matrix(length), *tiles)


def body(
    fine_waves,
    coarse_waves,
    coarse_kernel,
    row_valence,
    row_conduction,
    row_neighbours,
    row_weight_index,
    col_neighbours,
    col_weight_index,
    tile_list,
    weight_table,
):
    peers = lax.axis_size("ka")
    me = lax.axis_index("ka").astype(jnp.int32).reshape(1)
    fine_count = fine_waves.shape[0]
    held = coarse_waves.shape[0]

    always, needed = wave_blocks(peers)
    *packed, index = packed_waves(me, tile_list, coarse_waves, always + needed)
    arrived = []
    for block, (mask, _, _) in zip(packed, always):
        arrived.append(swapped(block, "ka", mask))

    own, _ = lax.optimization_barrier((coarse_kernel, packed[0]))
    upper = passed_along(own, "ga", -1)
    *tiles, scale = rotated_tiles(
        me,
        tile_list,
        (row_neighbours, row_weight_index, row_valence, row_conduction),
        (col_neighbours.T, col_weight_index.T),
        weight_table,
        own,
        upper,
    )
    if needed:
        index, tiles = lax.optimization_barrier((index[0], tiles))
        arrived += sent_where_needed(index, packed[len(always) :])
    tiles = [tiles[0]] + [swapped(tiles[mask], "ka", mask) for mask in range(1, peers)]
    partial = partial_correlations(
        me, tile_list, fine_waves, coarse_waves, always + needed, arrived
    )
    parts = lax.all_gather(partial, "ga")
    return finished(me, tile_list, parts, scale, tiles, held, fine_count)[None]


def solution(mesh):
    placed = (
        P("ka", None, "ga"),
        P("ka", None, "ga"),
        P("ga", None, "ka"),
        P("ga", None, None, None),
        P("ga", None, None, None),
        P("ga", None),
        P("ga", None),
        P("ka", None),
        P("ka", None),
        P(),
        P(),
    )
    return jax.shard_map(
        body, mesh=mesh, in_specs=placed, out_specs=P("ga", "ka", None), check_vma=False
    )
```

profile of v0, /device:TPU:0, one launch (start us, length us, event | category | flops | bytes accessed | tf_op | source)
XLA Modules:
  0.0 71.7 jit_solution(4548315652833114640)
XLA Ops:
  0.0 3.3 %pack.1 = (bf16[2,16,5120]{2,1,0:T(8,128)(2,1)}, bf16[2,16,5120]{2,1,0:T(8,128)(2,1)}, bf16[4,16,5120]{2,1,0:T(8,128)(2,1)}, bf16[2,16,5120]{2,1,0:T(8,128)(2,1)...) custom-call(s32[1]{0:T(128)} %bitcast.me_ref, s32[4,8]{1,0:T(4,128)} %list_ref.7, bf16[8,16,5120]{2,1,0:T(8,128)(2,1)} %own_ref.2), custom_call_target="tpu_custom_call" | custom-call | tf_op jit(solution)/shard_map/pack/pallas_call | solution.py:125
  3.3 3.1 %collective-permute-start.58 = (bf16[4,16,5120]{2,1,0:T(8,128)(2,1)}, bf16[4,16,5120]{2,1,0:T(8,128)(2,1)S(1)}, u32[]{:S(2)}, u32[]{:S(2)}) collective-permute-start(bf16[4,16,5120]{2,1,0:T(8,128)(2,1)} %get-tuple-element.228), channel_id=1, source_target_pairs={{0,1},{1,0},{2,3},{3,2},{4,5},{5,4},{6,7},{7,6},{8,9},{9,8},{10,11... | collective-permute-start | bytes 1966088 | tf_op jit(solution)/shard_map/ppermute | solution.py:38
  6.4 1.6 %collective-permute-start.59 = (bf16[6,64,512]{2,1,0:T(8,128)(2,1)}, bf16[6,64,512]{2,1,0:T(8,128)(2,1)S(1)}, u32[]{:S(2)}, u32[]{:S(2)}) collective-permute-start(bf16[6,64,512]{2,1,0:T(8,128)(2,1)} %own_ref.1), channel_id=1, source_target_pairs={{0,28},{4,0},{8,4},{12,8},{16,12},{20,16},{24,20},{28,24},{1,29},{... | collective-permute-start | bytes 1179656 | tf_op jit(solution)/shard_map/ppermute | solution.py:33
  8.0 2.5 %collective-permute-start.57 = (bf16[2,16,5120]{2,1,0:T(8,128)(2,1)}, bf16[2,16,5120]{2,1,0:T(8,128)(2,1)S(1)}, u32[]{:S(2)}, u32[]{:S(2)}) collective-permute-start(bf16[2,16,5120]{2,1,0:T(8,128)(2,1)} %get-tuple-element.227), channel_id=1, source_target_pairs={{0,3},{1,2},{2,1},{3,0},{4,7},{5,6},{6,5},{7,4},{8,11},{9,10},{10,... | collective-permute-start | bytes 983048 | tf_op jit(solution)/shard_map/ppermute | solution.py:38
  10.5 0.1 collective-permute-start.56
  10.6 3.0 %collective-permute-done.59.next_ref = bf16[6,64,512]{2,1,0:T(8,128)(2,1)S(1)} collective-permute-done((bf16[6,64,512]{2,1,0:T(8,128)(2,1)}, bf16[6,64,512]{2,1,0:T(8,128)(2,1)S(1)}, u32[]{:S(2)}, u32[]{:S(2)}) %collective-permute-start.59) | collective-permute-done | bytes 393248 | tf_op jit(solution)/shard_map/ppermute | solution.py:33
  13.7 0.0 copy-start.5
  13.7 0.8 %copy-done.5 = bf16[6,64,512]{2,1,0:T(8,128)(2,1)} copy-done((bf16[6,64,512]{2,1,0:T(8,128)(2,1)}, bf16[6,64,512]{2,1,0:T(8,128)(2,1)S(1)}, u32[]{:S(2)}) %copy-start.5) | copy-done | bytes 393240
  14.4 3.2 %rotate.1 = (bf16[64,256]{1,0:T(8,128)(2,1)}, bf16[64,256]{1,0:T(8,128)(2,1)}, bf16[64,256]{1,0:T(8,128)(2,1)}, bf16[64,256]{1,0:T(8,128)(2,1)}, f32[128,128]{1,0:T(8,128)}) custom-call(s32[1]{0:T(128)} %bitcast.me_ref, s32[4,8]{1,0:T(4,128)} %list_ref.7, s32[1,8]{1,0:T(1,128)} %near_ref.1, s32[1,8]{1,0:T(1,128)} %level_ref.1, f32[8]{0:T(128)} %table_ref.1, ...), custom_call_target="tpu_custom_call" | custom-call | tf_op jit(solution)/shard_map/rotate/pallas_call | solution.py:268
  18.3 0.0 copy-start.8
  18.3 0.0 copy-start.7
  18.3 0.0 copy-start.6
  18.3 0.0 copy-start
  18.4 0.0 copy-start.3
  18.4 30.4 %conditional.1 = ((bf16[2,16,5120]{2,1,0:T(8,128)(2,1)S(1)}, bf16[2,16,5120]{2,1,0:T(8,128)(2,1)S(1)})) conditional(s32[]{:T(128)} %clamp.3, (bf16[2,16,5120]{2,1,0:T(8,128)(2,1)S(1)}, bf16[2,16,5120]{2,1,0:T(8,128)(2,1)S(1)}) %tuple.144, (bf16[2,16,5120]{2,1,0:T(8,128)(2,1)S(1)}, ...), branch_computations={%region_0.0_spmd, %region_1.0_spmd, %region_2.0_spmd, %region_3.0_... | conditional | bytes 3932264 | solution.py:152
  18.4 4.6 %collective-permute-start.33 = (bf16[2,16,5120]{2,1,0:T(8,128)(2,1)S(1)}, bf16[2,16,5120]{2,1,0:T(8,128)(2,1)S(1)}, u32[]{:S(2)}, u32[]{:S(2)}) collective-permute-start(bf16[2,16,5120]{2,1,0:T(8,128)(2,1)S(1)} %get-tuple-element.183), channel_id=1, source_target_pairs={{2,0},{0,2},{6,4},{4,6},{10,8},{8,10},{14,12},{12,14},{18,16},{16,... | collective-permute-start | bytes 983048 | tf_op jit(solution)/shard_map/cond/branch_22_fun/ppermute | solution.py:148
  23.1 1.3 %collective-permute-start.34 = (bf16[2,16,5120]{2,1,0:T(8,128)(2,1)S(1)}, bf16[2,16,5120]{2,1,0:T(8,128)(2,1)S(1)}, u32[]{:S(2)}, u32[]{:S(2)}) collective-permute-start(bf16[2,16,5120]{2,1,0:T(8,128)(2,1)S(1)} %get-tuple-element.184), channel_id=1, source_target_pairs={{2,1},{0,3},{6,5},{4,7},{10,9},{8,11},{14,13},{12,15},{18,17},{16,... | collective-permute-start | bytes 983048 | tf_op jit(solution)/shard_map/cond/branch_22_fun/ppermute | solution.py:148
  24.4 22.7 %collective-permute-done.33 = bf16[2,16,5120]{2,1,0:T(8,128)(2,1)S(1)} collective-permute-done((bf16[2,16,5120]{2,1,0:T(8,128)(2,1)S(1)}, bf16[2,16,5120]{2,1,0:T(8,128)(2,1)S(1)}, u32[]{:S(2)}, u32[]{:S(2)}) %collective-permute-start.33) | collective-permute-done | bytes 327712 | tf_op jit(solution)/shard_map/cond/branch_22_fun/ppermute | solution.py:148
  47.1 1.7 %collective-permute-done.34 = bf16[2,16,5120]{2,1,0:T(8,128)(2,1)S(1)} collective-permute-done((bf16[2,16,5120]{2,1,0:T(8,128)(2,1)S(1)}, bf16[2,16,5120]{2,1,0:T(8,128)(2,1)S(1)}, u32[]{:S(2)}, u32[]{:S(2)}) %collective-permute-start.34) | collective-permute-done | bytes 327712 | tf_op jit(solution)/shard_map/cond/branch_22_fun/ppermute | solution.py:148
  48.8 0.0 copy-done.8
  48.8 4.6 %collective-permute-start.60 = (bf16[64,256]{1,0:T(8,128)(2,1)S(1)}, bf16[64,256]{1,0:T(8,128)(2,1)S(1)}, u32[]{:S(2)}, u32[]{:S(2)}) collective-permute-start(bf16[64,256]{1,0:T(8,128)(2,1)S(1)} %copy-done.8), channel_id=1, source_target_pairs={{0,1},{1,0},{2,3},{3,2},{4,5},{5,4},{6,7},{7,6},{8,9},{9,8},{10,11... | collective-permute-start | bytes 98312 | tf_op jit(solution)/shard_map/ppermute | solution.py:38
  53.5 0.0 copy-done.7
  53.5 0.3 collective-permute-start.61
  53.8 0.0 collective-permute-done.57.rest_1_
  53.8 0.0 copy-done.6
  53.8 2.1 %collective-permute-start.62 = (bf16[64,256]{1,0:T(8,128)(2,1)S(1)}, bf16[64,256]{1,0:T(8,128)(2,1)S(1)}, u32[]{:S(2)}, u32[]{:S(2)}) collective-permute-start(bf16[64,256]{1,0:T(8,128)(2,1)S(1)} %copy-done.6), channel_id=1, source_target_pairs={{0,3},{1,2},{2,1},{3,0},{4,7},{5,6},{6,5},{7,4},{8,11},{9,10},{10,... | collective-permute-start | bytes 98312 | tf_op jit(solution)/shard_map/ppermute | solution.py:38
  55.9 0.0 collective-permute-done.56.rest_0_
  55.9 0.0 collective-permute-done.58.rest_2_
  55.9 0.0 copy-done
  55.9 0.0 copy-done.3
  55.9 0.0 copy-start.1
  55.9 0.0 copy-start.2
  56.0 0.0 copy-start.4
  56.0 3.6 %correlate.1 = f32[128,128]{1,0:T(8,128)S(1)} custom-call(s32[1]{0:T(128)} %bitcast.me_ref, s32[4,8]{1,0:T(4,128)S(1)} %copy-done.3, bf16[16,16,5120]{2,1,0:T(8,128)(2,1)} %fine_hbm.1, bf16[8,16,5120]{2,1,0:T(8,128)(2,1)S(1)} %copy-done, bf16[2,16,5120]{2,1,0:T(8,128)(2,1)S(1)} %collective-permute-done.56.rest_0_, ...), custom_call_target="tpu_custom_call" | custom-call | tf_op jit(solution)/shard_map/correlate/pallas_call | solution.py:337
  59.5 9.9 %all-gather = f32[1024,128]{1,0:T(8,128)S(1)} all-gather(f32[128,128]{1,0:T(8,128)S(1)} %correlate.1), channel_id=2, replica_groups=mesh['ga'=8,'ka'=4] {'ga'}, dimensions={0}, use_global_device_ids=true | all-gather | bytes 589824 | tf_op jit(solution)/shard_map/all_gather | solution.py:472
  69.4 0.0 collective-permute-done.60.rest_1_
  69.4 0.0 collective-permute-done.61.rest_2_
  69.4 0.0 collective-permute-done.62.rest_3_
  69.4 0.0 copy-done.1
  69.4 0.0 copy-done.2
  69.4 0.0 copy-done.4
  69.4 2.2 %finish.1 = bf16[16,4096]{1,0:T(8,128)(2,1)} custom-call(s32[1]{0:T(128)} %bitcast.me_ref, s32[4,8]{1,0:T(4,128)S(1)} %copy-done.3, f32[8,128,128]{2,1,0:T(8,128)S(1)} %bitcast.6, f32[128,128]{1,0:T(8,128)S(1)} %copy-done.2, bf16[128,1024]{1,0:T(8,128)(2,1)S(1)} %copy-done.1, bf16[64,256]{1,0:T(8,128)(2,1)S(1)} %copy-done.4, ...), custom_call_target="tpu_custom_call" | custom-call | tf_op jit(solution)/shard_map/finish/pallas_call | solution.py:413
  (2 shorter events, 0.0 us)
Async XLA Ops:
  3.3 52.6 %collective-permute-start.58 = (bf16[4,16,5120]{2,1,0:T(8,128)(2,1)}, bf16[4,16,5120]{2,1,0:T(8,128)(2,1)S(1)}, u32[]{:S(2)}, u32[]{:S(2)}) collective-permute-start(bf16[4,16,5120]{2,1,0:T(8,128)(2,1)} %get-tuple-element.228), channel_id=1, source_target_pairs={{0,1},{1,0},{2,3},{3,2},{4,5},{5,4},{6,7},{7,6},{8,9},{9,8},{10,11... | collective-permute-start | bytes 1966088 | tf_op jit(solution)/shard_map/ppermute | solution.py:38
  6.4 7.2 %collective-permute-start.59 = (bf16[6,64,512]{2,1,0:T(8,128)(2,1)}, bf16[6,64,512]{2,1,0:T(8,128)(2,1)S(1)}, u32[]{:S(2)}, u32[]{:S(2)}) collective-permute-start(bf16[6,64,512]{2,1,0:T(8,128)(2,1)} %own_ref.1), channel_id=1, source_target_pairs={{0,28},{4,0},{8,4},{12,8},{16,12},{20,16},{24,20},{28,24},{1,29},{... | collective-permute-start | bytes 1179656 | tf_op jit(solution)/shard_map/ppermute | solution.py:33
  8.0 45.8 %collective-permute-start.57 = (bf16[2,16,5120]{2,1,0:T(8,128)(2,1)}, bf16[2,16,5120]{2,1,0:T(8,128)(2,1)S(1)}, u32[]{:S(2)}, u32[]{:S(2)}) collective-permute-start(bf16[2,16,5120]{2,1,0:T(8,128)(2,1)} %get-tuple-element.227), channel_id=1, source_target_pairs={{0,3},{1,2},{2,1},{3,0},{4,7},{5,6},{6,5},{7,4},{8,11},{9,10},{10,... | collective-permute-start | bytes 983048 | tf_op jit(solution)/shard_map/ppermute | solution.py:38
  10.5 45.4 %collective-permute-start.56 = (bf16[2,16,5120]{2,1,0:T(8,128)(2,1)}, bf16[2,16,5120]{2,1,0:T(8,128)(2,1)S(1)}, u32[]{:S(2)}, u32[]{:S(2)}) collective-permute-start(bf16[2,16,5120]{2,1,0:T(8,128)(2,1)} %get-tuple-element.226), channel_id=1, source_target_pairs={{0,2},{1,3},{2,0},{3,1},{4,6},{5,7},{6,4},{7,5},{8,10},{9,11},{10,... | collective-permute-start | bytes 983048 | tf_op jit(solution)/shard_map/ppermute | solution.py:38
  13.7 0.8 %copy-start.5 = (bf16[6,64,512]{2,1,0:T(8,128)(2,1)}, bf16[6,64,512]{2,1,0:T(8,128)(2,1)S(1)}, u32[]{:S(2)}) copy-start(bf16[6,64,512]{2,1,0:T(8,128)(2,1)S(1)} %collective-permute-done.59.next_ref) | copy-start | bytes 1179652
  18.3 30.5 %copy-start.8 = (bf16[64,256]{1,0:T(8,128)(2,1)S(1)}, bf16[64,256]{1,0:T(8,128)(2,1)}, u32[]{:S(2)}) copy-start(bf16[64,256]{1,0:T(8,128)(2,1)} %get-tuple-element.242) | copy-start | bytes 98308
  18.3 35.1 %copy-start.7 = (bf16[64,256]{1,0:T(8,128)(2,1)S(1)}, bf16[64,256]{1,0:T(8,128)(2,1)}, u32[]{:S(2)}) copy-start(bf16[64,256]{1,0:T(8,128)(2,1)} %get-tuple-element.243) | copy-start | bytes 98308
  18.3 35.5 %copy-start.6 = (bf16[64,256]{1,0:T(8,128)(2,1)S(1)}, bf16[64,256]{1,0:T(8,128)(2,1)}, u32[]{:S(2)}) copy-start(bf16[64,256]{1,0:T(8,128)(2,1)} %get-tuple-element.244) | copy-start | bytes 98308
  18.3 37.6 %copy-start = (bf16[8,16,5120]{2,1,0:T(8,128)(2,1)S(1)}, bf16[8,16,5120]{2,1,0:T(8,128)(2,1)}, u32[]{:S(2)}) copy-start(bf16[8,16,5120]{2,1,0:T(8,128)(2,1)} %own_ref.2) | copy-start | bytes 3932164
  18.4 37.6 %copy-start.3 = (s32[4,8]{1,0:T(4,128)S(1)}, s32[4,8]{1,0:T(4,128)}, u32[]{:S(2)}) copy-start(s32[4,8]{1,0:T(4,128)} %list_ref.7) | copy-start | bytes 388
  18.4 28.7 %collective-permute-start.33 = (bf16[2,16,5120]{2,1,0:T(8,128)(2,1)S(1)}, bf16[2,16,5120]{2,1,0:T(8,128)(2,1)S(1)}, u32[]{:S(2)}, u32[]{:S(2)}) collective-permute-start(bf16[2,16,5120]{2,1,0:T(8,128)(2,1)S(1)} %get-tuple-element.183), channel_id=1, source_target_pairs={{2,0},{0,2},{6,4},{4,6},{10,8},{8,10},{14,12},{12,14},{18,16},{16,... | collective-permute-start | bytes 983048 | tf_op jit(solution)/shard_map/cond/branch_22_fun/ppermute | solution.py:148
  23.1 25.7 %collective-permute-start.34 = (bf16[2,16,5120]{2,1,0:T(8,128)(2,1)S(1)}, bf16[2,16,5120]{2,1,0:T(8,128)(2,1)S(1)}, u32[]{:S(2)}, u32[]{:S(2)}) collective-permute-start(bf16[2,16,5120]{2,1,0:T(8,128)(2,1)S(1)} %get-tuple-element.184), channel_id=1, source_target_pairs={{2,1},{0,3},{6,5},{4,7},{10,9},{8,11},{14,13},{12,15},{18,17},{16,... | collective-permute-start | bytes 983048 | tf_op jit(solution)/shard_map/cond/branch_22_fun/ppermute | solution.py:148
  48.8 20.6 %collective-permute-start.60 = (bf16[64,256]{1,0:T(8,128)(2,1)S(1)}, bf16[64,256]{1,0:T(8,128)(2,1)S(1)}, u32[]{:S(2)}, u32[]{:S(2)}) collective-permute-start(bf16[64,256]{1,0:T(8,128)(2,1)S(1)} %copy-done.8), channel_id=1, source_target_pairs={{0,1},{1,0},{2,3},{3,2},{4,5},{5,4},{6,7},{7,6},{8,9},{9,8},{10,11... | collective-permute-start | bytes 98312 | tf_op jit(solution)/shard_map/ppermute | solution.py:38
  53.5 15.9 %collective-permute-start.61 = (bf16[64,256]{1,0:T(8,128)(2,1)S(1)}, bf16[64,256]{1,0:T(8,128)(2,1)S(1)}, u32[]{:S(2)}, u32[]{:S(2)}) collective-permute-start(bf16[64,256]{1,0:T(8,128)(2,1)S(1)} %copy-done.7), channel_id=1, source_target_pairs={{0,2},{1,3},{2,0},{3,1},{4,6},{5,7},{6,4},{7,5},{8,10},{9,11},{10,... | collective-permute-start | bytes 98312 | tf_op jit(solution)/shard_map/ppermute | solution.py:38
  53.8 15.6 %collective-permute-start.62 = (bf16[64,256]{1,0:T(8,128)(2,1)S(1)}, bf16[64,256]{1,0:T(8,128)(2,1)S(1)}, u32[]{:S(2)}, u32[]{:S(2)}) collective-permute-start(bf16[64,256]{1,0:T(8,128)(2,1)S(1)} %copy-done.6), channel_id=1, source_target_pairs={{0,3},{1,2},{2,1},{3,0},{4,7},{5,6},{6,5},{7,4},{8,11},{9,10},{10,... | collective-permute-start | bytes 98312 | tf_op jit(solution)/shard_map/ppermute | solution.py:38
  55.9 13.5 %copy-start.1 = (bf16[128,1024]{1,0:T(8,128)(2,1)S(1)}, bf16[128,1024]{1,0:T(8,128)(2,1)}, u32[]{:S(2)}) copy-start(bf16[128,1024]{1,0:T(8,128)(2,1)} %constant.10.clone.spread_ref) | copy-start | bytes 786436
  55.9 13.5 %copy-start.2 = (f32[128,128]{1,0:T(8,128)S(1)}, f32[128,128]{1,0:T(8,128)}, u32[]{:S(2)}) copy-start(f32[128,128]{1,0:T(8,128)} %get-tuple-element.240.scale_ref) | copy-start | bytes 196612
  56.0 13.5 %copy-start.4 = (bf16[64,256]{1,0:T(8,128)(2,1)S(1)}, bf16[64,256]{1,0:T(8,128)(2,1)}, u32[]{:S(2)}) copy-start(bf16[64,256]{1,0:T(8,128)(2,1)} %get-tuple-element.241.rest_0_) | copy-start | bytes 98308
where the time goes:
time: 71.9 us; the launch traced here: 71.7 us
  waiting for transfers between devices  27.4 us (38%)
  starting transfers between devices  20.3 us (28%)
  Pallas kernels  12.3 us (17%)
  blocking collectives  9.86 us (14%)
  local copies, waits for them, and re-layouts  0.85 us (1%)
  between operations  0.84 us (1%)
    ppermute x2, waiting for transfers between devices, sending(): lax.ppermute(packed[which], 'ka', pairs)  24.4 us
    ppermute x6, starting transfers between devices, swapped(): return lax.ppermute(array, axis, [(i, i ^ mask) for i in range(peers)])  12.8 us
    all_gather x1, blocking collectives, body(): parts = lax.all_gather(partial, 'ga')  9.86 us
    ppermute x2, starting transfers between devices, sending(): lax.ppermute(packed[which], 'ka', pairs)  5.94 us
    pallas_call x1, Pallas kernels, partial_correlations(): pl.pallas_call(functools.partial(correlate_kernel, blocks), out_shape=jax...  3.55 us
    pallas_call x1, Pallas kernels, packed_waves(): pl.pallas_call(functools.partial(pack_kernel, blocks), out_shape=shapes +...  3.31 us
    pallas_call x1, Pallas kernels, rotated_tiles(): pl.pallas_call(functools.partial(rotate_kernel, peers), out_shape=[block]...  3.19 us
    ppermute x1, waiting for transfers between devices, passed_along(): lax.ppermute(array, axis, [(i, (i + by) % peers) for i in range(peers)])  3.02 us
  transfers between devices with their start and end apart: 9, of which 3 were waited for; matrix products, arithmetic and copies ran while one was open for 0% of the time, Pallas kernels for 9%

commit v1 on v0

--- a/solution.py
+++ b/solution.py
@@ -94,10 +94,11 @@
 
 
 def pack_kernel(blocks, me_ref, list_ref, waves_ref, *rest):
-    outs, index_ref, sems = rest[:-2], rest[-2], rest[-1]
+    outs, rest = rest[: len(blocks)], rest[len(blocks) :]
+    *index_ref, buffer, in_sems, out_sems = rest
     held = waves_ref.shape[0]
     me = me_ref[0]
-    copies = []
+    ins, stores = [], []
     slots = {}
     for (mask, low, high), out in zip(blocks, outs):
         if mask not in slots:
@@ -105,29 +106,42 @@
                 list_ref, lax.bitwise_xor(me, mask), me, held, SLOT_COUNT
             )
         for slot in range(low, high):
+            at = len(ins)
             copy = pltpu.make_async_copy(
-                waves_ref.at[slots[mask][slot]], out.at[slot - low], sems.at[len(copies)]
+                waves_ref.at[slots[mask][slot]], buffer.at[at], in_sems.at[at]
             )
             copy.start()
-            copies.append(copy)
-    index_ref[0] = later_index(list_ref, held) if list_ref.shape[0] == 4 else jnp.int32(0)
-    for copy in copies:
+            ins.append(copy)
+            stores.append(
+                pltpu.make_async_copy(buffer.at[at], out.at[slot - low], out_sems.at[at])
+            )
+    for ref in index_ref:
+        ref[0] = later_index(list_ref, held)
+    for copy, store in zip(ins, stores):
         copy.wait()
-
-
-def packed_waves(me, tile_list, coarse_waves, blocks):
+        store.start()
+    for store in stores:
+        store.wait()
+
+
+def packed_waves(me, tile_list, coarse_waves, blocks, with_index):
     _, bands, waves = coarse_waves.shape
     shapes = [
         jax.ShapeDtypeStruct((high - low, bands, waves), coarse_waves.dtype)
         for _, low, high in blocks
     ]
     copies = sum(high - low for _, low, high in blocks)
+    index = [jax.ShapeDtypeStruct((1,), jnp.int32)] if with_index else []
     return pl.pallas_call(
         functools.partial(pack_kernel, blocks),
-        out_shape=shapes + [jax.ShapeDtypeStruct((1,), jnp.int32)],
-        in_specs=[SMEM, SMEM, VMEM],
-        out_specs=[ANY] * len(blocks) + [SMEM],
-        scratch_shapes=[pltpu.SemaphoreType.DMA((copies,))],
+        out_shape=shapes + index,
+        in_specs=[SMEM, SMEM, ANY],
+        out_specs=[ANY] * len(blocks) + [SMEM] * len(index),
+        scratch_shapes=[
+            pltpu.VMEM((copies, bands, waves), coarse_waves.dtype),
+            pltpu.SemaphoreType.DMA((copies,)),
+            pltpu.SemaphoreType.DMA((copies,)),
+        ],
         name="pack",
     )(me, tile_list, coarse_waves)
 
@@ -291,20 +305,17 @@
     return entries
 
 
-def correlate_kernel(blocks, me_ref, list_ref, fine_hbm, own_ref, *rest):
-    arrived, (out_ref, fine, listed, sems) = rest[: len(blocks)], rest[len(blocks) :]
+def correlate_kernel(peers, blocks, me_ref, list_ref, fine_hbm, own_ref, *rest):
+    arrived, rest = rest[: len(blocks)], rest[len(blocks) :]
+    tiles_in, (out_ref, left_ref, fine, listed, tiles, sem) = rest[:peers], rest[peers:]
     held = own_ref.shape[0]
     me = me_ref[0]
     fine_count, bands, waves = fine_hbm.shape
     length = listed.shape[0]
-    parts = sems.shape[0]
-    count = fine_count // parts
-    copies = []
-    for part in range(parts):
-        some = pl.ds(part * count, count)
-        copies.append(pltpu.make_async_copy(fine_hbm.at[some], fine.at[some], sems.at[part]))
-        copies[-1].start()
-    for place, (column, mask, rank) in enumerate(list_places(list_ref, me, held)):
+    copy = pltpu.make_async_copy(fine_hbm, fine, sem)
+    copy.start()
+    entries = list_places(list_ref, me, held)
+    for place, (column, mask, rank) in enumerate(entries):
 
         def fetch(source, at, place=place):
             listed[place] = source[at]
@@ -315,34 +326,46 @@
             pl.when(jnp.logical_and(mask == other, here))(
                 functools.partial(fetch, source, rank - low)
             )
-    for part in range(parts):
-        copies[part].wait()
-        dense = lax.dot_general(
-            fine[part * count : (part + 1) * count].reshape(count * bands, waves),
-            listed[...].reshape(length * bands, waves),
-            (((1,), (1,)), ((), ())),
-            preferred_element_type=jnp.float32,
-        )
-        dense = dense.reshape(count, 2, VALENCE, length * bands)
-        lanes = lax.broadcasted_iota(jnp.int32, (count, VALENCE, length * bands), 2)
-        both = jnp.where(lanes % bands < VALENCE, dense[:, 0], dense[:, 1])
-        out_ref[pl.ds(part * count * VALENCE, count * VALENCE), :] = both.reshape(
-            count * VALENCE, length * bands
-        )
-
-
-def partial_correlations(me, tile_list, fine_waves, coarse_waves, blocks, arrived):
+    for mask in range(peers):
+        tiles[mask] = tiles_in[mask][...]
+    for place, (_, mask, rank) in enumerate(entries):
+        block = tiles[mask]
+        tile = block[:, :BAND_PAIRS]
+        for slot in range(1, SLOT_COUNT):
+            tile = jnp.where(
+                rank == slot, block[:, slot * BAND_PAIRS : (slot + 1) * BAND_PAIRS], tile
+            )
+        left_ref[:, place * BAND_PAIRS : (place + 1) * BAND_PAIRS] = tile
+    copy.wait()
+    dense = lax.dot_general(
+        fine[...].reshape(fine_count * bands, waves),
+        listed[...].reshape(length * bands, waves),
+        (((1,), (1,)), ((), ())),
+        preferred_element_type=jnp.float32,
+    )
+    dense = dense.reshape(fine_count, 2, VALENCE, length * bands)
+    lanes = lax.broadcasted_iota(jnp.int32, (fine_count, VALENCE, length * bands), 2)
+    both = jnp.where(lanes % bands < VALENCE, dense[:, 0], dense[:, 1])
+    out_ref[...] = both.reshape(fine_count * VALENCE, length * bands)
+
+
+def partial_correlations(me, tile_list, fine_waves, coarse_waves, blocks, arrived, tiles):
     fine_count, bands, waves = fine_waves.shape
     length = tile_list.shape[1]
+    peers = len(tiles)
     return pl.pallas_call(
-        functools.partial(correlate_kernel, blocks),
-        out_shape=jax.ShapeDtypeStruct((fine_count * VALENCE, length * bands), jnp.float32),
-        in_specs=[SMEM, SMEM, ANY] + [VMEM] * (1 + len(blocks)),
-        out_specs=VMEM,
+        functools.partial(correlate_kernel, peers, blocks),
+        out_shape=[
+            jax.ShapeDtypeStruct((fine_count * VALENCE, length * bands), jnp.float32),
+            jax.ShapeDtypeStruct((BAND_PAIRS, length * BAND_PAIRS), jnp.bfloat16),
+        ],
+        in_specs=[SMEM, SMEM, ANY] + [VMEM] * (1 + len(blocks) + peers),
+        out_specs=[VMEM, VMEM],
         scratch_shapes=[
             pltpu.VMEM((fine_count, bands, waves), jnp.bfloat16),
             pltpu.VMEM((length, bands, waves), jnp.bfloat16),
-            pltpu.SemaphoreType.DMA((2 if fine_count % 2 == 0 else 1,)),
+            pltpu.VMEM((peers, BAND_PAIRS, SLOT_COUNT * BAND_PAIRS), jnp.bfloat16),
+            pltpu.SemaphoreType.DMA(()),
         ],
         compiler_params=LIMIT,
         name="correlate",
@@ -352,26 +375,13 @@
         pltpu.with_memory_space_constraint(fine_waves, pltpu.HBM),
         coarse_waves,
         *arrived,
-    )
-
-
-def finish_kernel(peers, held, me_ref, list_ref, parts_ref, scale_ref, spread_ref, *rest):
-    tiles_in, (out_ref, tiles, left, wide, rotation, blocks) = rest[:peers], rest[peers:]
-    me = me_ref[0]
+        *tiles,
+    )
+
+
+def finish_kernel(parts_ref, scale_ref, spread_ref, left, out_ref, wide, rotation, blocks):
     fine_count = out_ref.shape[0]
-    length = list_ref.shape[1]
-    width = length * BAND_PAIRS
-    for mask in range(peers):
-        tiles[mask] = tiles_in[mask][...]
-    for place, (column, mask, rank) in enumerate(list_places(list_ref, me, held)):
-        block = tiles[mask]
-        tile = block[:, :BAND_PAIRS]
-        for slot in range(1, SLOT_COUNT):
-            tile = jnp.where(
-                rank == slot, block[:, slot * BAND_PAIRS : (slot + 1) * BAND_PAIRS], tile
-            )
-        left[:, place * BAND_PAIRS : (place + 1) * BAND_PAIRS] = tile
-
+    width = left.shape[1]
     total = jnp.sum(parts_ref[...], axis=0) * scale_ref[...]
     wide[...] = split_dot(total, spread_ref[...])
 
@@ -407,24 +417,21 @@
     return jnp.asarray(np.concatenate([valence, conduction], axis=1), dtype=jnp.bfloat16)
 
 
-def finished(me, tile_list, parts, scale, tiles, held, fine_count):
-    length = tile_list.shape[1]
-    peers = len(tiles)
+def finished(parts, scale, left, fine_count):
+    width = left.shape[1]
     return pl.pallas_call(
-        functools.partial(finish_kernel, peers, held),
+        finish_kernel,
         out_shape=jax.ShapeDtypeStruct((fine_count, BAND_PAIRS * BAND_PAIRS), jnp.bfloat16),
-        in_specs=[SMEM, SMEM] + [VMEM] * (3 + peers),
+        in_specs=[VMEM] * 4,
         out_specs=VMEM,
         scratch_shapes=[
-            pltpu.VMEM((peers, BAND_PAIRS, SLOT_COUNT * BAND_PAIRS), jnp.bfloat16),
-            pltpu.VMEM((BAND_PAIRS, length * BAND_PAIRS), jnp.bfloat16),
-            pltpu.VMEM((fine_count * VALENCE, 2 * length * BAND_PAIRS), jnp.float32),
-            pltpu.VMEM((fine_count * BAND_PAIRS, length * BAND_PAIRS), jnp.bfloat16),
+            pltpu.VMEM((fine_count * VALENCE, 2 * width), jnp.float32),
+            pltpu.VMEM((fine_count * BAND_PAIRS, width), jnp.bfloat16),
             pltpu.VMEM((fine_count * BAND_PAIRS, BAND_PAIRS), jnp.float32),
         ],
         compiler_params=LIMIT,
         name="finish",
-    )(me, tile_list, parts, scale, spread_matrix(length), *tiles)
+    )(parts, scale, spread_matrix(width // BAND_PAIRS), left)
 
 
 def body(
@@ -442,16 +449,18 @@
 ):
     peers = lax.axis_size("ka")
     me = lax.axis_index("ka").astype(jnp.int32).reshape(1)
-    fine_count = fine_waves.shape[0]
-    held = coarse_waves.shape[0]
 
     always, needed = wave_blocks(peers)
-    *packed, index = packed_waves(me, tile_list, coarse_waves, always + needed)
+    early = len(FAR) if needed else 1
+    packed = packed_waves(me, tile_list, coarse_waves, always[:early], False)
+    own, later_list, _ = lax.optimization_barrier((coarse_kernel, tile_list, packed[0]))
+    packed += packed_waves(
+        me, later_list, coarse_waves, always[early:] + needed, with_index=bool(needed)
+    )
     arrived = []
-    for block, (mask, _, _) in zip(packed, always):
-        arrived.append(swapped(block, "ka", mask))
-
-    own, _ = lax.optimization_barrier((coarse_kernel, packed[0]))
+    for place, (mask, _, _) in enumerate(always):
+        arrived.append(swapped(packed[place], "ka", mask))
+
     upper = passed_along(own, "ga", -1)
     *tiles, scale = rotated_tiles(
         me,
@@ -463,14 +472,14 @@
         upper,
     )
     if needed:
-        index, tiles = lax.optimization_barrier((index[0], tiles))
-        arrived += sent_where_needed(index, packed[len(always) :])
+        index, tiles = lax.optimization_barrier((packed[-1][0], tiles))
+        arrived += sent_where_needed(index, packed[len(always) : -1])
     tiles = [tiles[0]] + [swapped(tiles[mask], "ka", mask) for mask in range(1, peers)]
-    partial = partial_correlations(
-        me, tile_list, fine_waves, coarse_waves, always + needed, arrived
+    partial, left = partial_correlations(
+        me, tile_list, fine_waves, coarse_waves, always + needed, arrived, tiles
     )
     parts = lax.all_gather(partial, "ga")
-    return finished(me, tile_list, parts, scale, tiles, held, fine_count)[None]
+    return finished(parts, scale, left, fine_waves.shape[0])[None]
 
 
 def solution(mesh):

time: 71.9 us -> 77.8 us (1.082)
  waiting for transfers between devices: 27.4 us -> 30.6 us
  Pallas kernels: 12.3 us -> 14.4 us
    ppermute x6, waiting for transfers between devices: 0.02 us -> 3.46 us  [swapped(): return lax.ppermute(array, axis, [(i, i ^ mask) for i in range(peers)])]
    pallas_call x1 -> x2, Pallas kernels: 3.31 us -> 6.38 us  [packed_waves(): pl.pallas_call(functools.partial(pack_kernel, blocks), out_shape=shapes +...]
    pallas_call x2, Pallas kernels: 5.79 us -> 4.82 us  [the longest x1 3.16 us: partial_correlations(): pl.pallas_call(functools.partial(correlate_kernel, peers, blocks), out_sh...]
  transfers between devices with their start and end apart: 9 -> 9, of which waited for: 3 -> 5; matrix products, arithmetic and copies ran while one was open for 0% -> 0% of each run, Pallas kernels for 9% -> 4%
where the time goes in v1:
time: 77.8 us; the launch traced here: 77.5 us
  waiting for transfers between devices  30.6 us (39%)
  starting transfers between devices  21 us (27%)
  Pallas kernels  14.4 us (19%)
  blocking collectives  9.86 us (13%)
  local copies, waits for them, and re-layouts  0.86 us (1%)
    ppermute x2, waiting for transfers between devices, sending(): lax.ppermute(packed[which], 'ka', pairs)  24.6 us
    ppermute x6, starting transfers between devices, swapped(): return lax.ppermute(array, axis, [(i, i ^ mask) for i in range(peers)])  13.3 us
    all_gather x1, blocking collectives, body(): parts = lax.all_gather(partial, 'ga')  9.86 us
    pallas_call x2, Pallas kernels, packed_waves(): pl.pallas_call(functools.partial(pack_kernel, blocks), out_shape=shapes +...  6.38 us
    ppermute x2, starting transfers between devices, sending(): lax.ppermute(packed[which], 'ka', pairs)  6.12 us
    ppermute x6, waiting for transfers between devices, swapped(): return lax.ppermute(array, axis, [(i, i ^ mask) for i in range(peers)])  3.46 us
    pallas_call x1, Pallas kernels, rotated_tiles(): pl.pallas_call(functools.partial(rotate_kernel, peers), out_shape=[block]...  3.19 us
    pallas_call x1, Pallas kernels, partial_correlations(): pl.pallas_call(functools.partial(correlate_kernel, peers, blocks), out_sh...  3.16 us
  transfers between devices with their start and end apart: 9, of which 5 were waited for; matrix products, arithmetic and copies ran while one was open for 0% of the time, Pallas kernels for 4%

profile of v1, /device:TPU:0, one launch (start us, length us, event | category | flops | bytes accessed | tf_op | source)
XLA Modules:
  0.0 77.5 jit_solution(11820837090483090852)
XLA Ops:
  0.0 0.0 copy-start.5
  0.0 2.7 %pack.2 = (bf16[2,16,5120]{2,1,0:T(8,128)(2,1)}, bf16[2,16,5120]{2,1,0:T(8,128)(2,1)}) custom-call(s32[1]{0:T(128)} %bitcast.me_ref, s32[4,8]{1,0:T(4,128)} %list_ref.6, bf16[8,16,5120]{2,1,0:T(8,128)(2,1)} %own_ref.2), custom_call_target="tpu_custom_call" | custom-call | tf_op jit(solution)/shard_map/pack/pallas_call | solution.py:135
  2.8 3.6 %pack.3 = (bf16[4,16,5120]{2,1,0:T(8,128)(2,1)}, bf16[2,16,5120]{2,1,0:T(8,128)(2,1)S(1)}, bf16[2,16,5120]{2,1,0:T(8,128)(2,1)S(1)}, s32[1]{0:T(128)}) custom-call(s32[1]{0:T(128)} %bitcast.me_ref, s32[4,8]{1,0:T(4,128)} %list_ref.6, bf16[8,16,5120]{2,1,0:T(8,128)(2,1)} %own_ref.2), custom_call_target="tpu_custom_call" | custom-call | tf_op jit(solution)/shard_map/pack/pallas_call | solution.py:135
  6.4 3.3 %collective-permute-start.58 = (bf16[4,16,5120]{2,1,0:T(8,128)(2,1)}, bf16[4,16,5120]{2,1,0:T(8,128)(2,1)S(1)}, u32[]{:S(2)}, u32[]{:S(2)}) collective-permute-start(bf16[4,16,5120]{2,1,0:T(8,128)(2,1)} %get-tuple-element.232), channel_id=1, source_target_pairs={{0,1},{1,0},{2,3},{3,2},{4,5},{5,4},{6,7},{7,6},{8,9},{9,8},{10,11... | collective-permute-start | bytes 1966088 | tf_op jit(solution)/shard_map/ppermute | solution.py:38
  9.7 0.0 copy-done.5
  9.7 1.6 %collective-permute-start.59 = (bf16[6,64,512]{2,1,0:T(8,128)(2,1)S(1)}, bf16[6,64,512]{2,1,0:T(8,128)(2,1)S(1)}, u32[]{:S(2)}, u32[]{:S(2)}) collective-permute-start(bf16[6,64,512]{2,1,0:T(8,128)(2,1)S(1)} %copy-done.5), channel_id=1, source_target_pairs={{0,28},{4,0},{8,4},{12,8},{16,12},{20,16},{24,20},{28,24},{1,29},{... | collective-permute-start | bytes 1179656 | tf_op jit(solution)/shard_map/ppermute | solution.py:33
  11.3 2.8 %collective-permute-start.56 = (bf16[2,16,5120]{2,1,0:T(8,128)(2,1)}, bf16[2,16,5120]{2,1,0:T(8,128)(2,1)S(1)}, u32[]{:S(2)}, u32[]{:S(2)}) collective-permute-start(bf16[2,16,5120]{2,1,0:T(8,128)(2,1)} %get-tuple-element.229), channel_id=1, source_target_pairs={{0,2},{1,3},{2,0},{3,1},{4,6},{5,7},{6,4},{7,5},{8,10},{9,11},{10,... | collective-permute-start | bytes 983048 | tf_op jit(solution)/shard_map/ppermute | solution.py:38
  14.0 0.0 collective-permute-start.57
  14.0 2.5 %collective-permute-done.59.next_ref = bf16[6,64,512]{2,1,0:T(8,128)(2,1)S(1)} collective-permute-done((bf16[6,64,512]{2,1,0:T(8,128)(2,1)S(1)}, bf16[6,64,512]{2,1,0:T(8,128)(2,1)S(1)}, u32[]{:S(2)}, u32[]{:S(2)}) %collective-permute-start.59) | collective-permute-done | bytes 393248 | tf_op jit(solution)/shard_map/ppermute | solution.py:33
  16.6 0.0 copy-start.6
  16.6 0.8 copy-done.6
  17.3 3.2 %rotate.1 = (bf16[64,256]{1,0:T(8,128)(2,1)}, bf16[64,256]{1,0:T(8,128)(2,1)}, bf16[64,256]{1,0:T(8,128)(2,1)}, bf16[64,256]{1,0:T(8,128)(2,1)}, f32[128,128]{1,0:T(8,128)}) custom-call(s32[1]{0:T(128)} %bitcast.me_ref, s32[4,8]{1,0:T(4,128)} %list_ref.6, s32[1,8]{1,0:T(1,128)} %near_ref.1, s32[1,8]{1,0:T(1,128)} %level_ref.1, f32[8]{0:T(128)} %table_ref.1, ...), custom_call_target="tpu_custom_call" | custom-call | tf_op jit(solution)/shard_map/rotate/pallas_call | solution.py:282
  21.1 0.0 copy-start.9
  21.2 0.0 copy-start.8
  21.2 0.0 copy-start.7
  21.2 0.0 copy-start
  21.2 0.0 copy-start.3
  21.2 0.0 copy-start.4
  21.2 30.9 %conditional.1 = ((bf16[2,16,5120]{2,1,0:T(8,128)(2,1)S(1)}, bf16[2,16,5120]{2,1,0:T(8,128)(2,1)S(1)})) conditional(s32[]{:T(128)} %clamp.3, (bf16[2,16,5120]{2,1,0:T(8,128)(2,1)S(1)}, bf16[2,16,5120]{2,1,0:T(8,128)(2,1)S(1)}) %tuple.144, (bf16[2,16,5120]{2,1,0:T(8,128)(2,1)S(1)}, ...), branch_computations={%region_0.0_spmd, %region_1.0_spmd, %region_2.0_spmd, %region_3.0_... | conditional | bytes 3932264 | solution.py:166
  21.3 4.8 %collective-permute-start.33 = (bf16[2,16,5120]{2,1,0:T(8,128)(2,1)S(1)}, bf16[2,16,5120]{2,1,0:T(8,128)(2,1)S(1)}, u32[]{:S(2)}, u32[]{:S(2)}) collective-permute-start(bf16[2,16,5120]{2,1,0:T(8,128)(2,1)S(1)} %get-tuple-element.183), channel_id=1, source_target_pairs={{2,0},{0,2},{6,4},{4,6},{10,8},{8,10},{14,12},{12,14},{18,16},{16,... | collective-permute-start | bytes 983048 | tf_op jit(solution)/shard_map/cond/branch_22_fun/ppermute | solution.py:162
  26.1 1.3 %collective-permute-start.34 = (bf16[2,16,5120]{2,1,0:T(8,128)(2,1)S(1)}, bf16[2,16,5120]{2,1,0:T(8,128)(2,1)S(1)}, u32[]{:S(2)}, u32[]{:S(2)}) collective-permute-start(bf16[2,16,5120]{2,1,0:T(8,128)(2,1)S(1)} %get-tuple-element.184), channel_id=1, source_target_pairs={{2,1},{0,3},{6,5},{4,7},{10,9},{8,11},{14,13},{12,15},{18,17},{16,... | collective-permute-start | bytes 983048 | tf_op jit(solution)/shard_map/cond/branch_22_fun/ppermute | solution.py:162
  27.4 23.3 %collective-permute-done.33 = bf16[2,16,5120]{2,1,0:T(8,128)(2,1)S(1)} collective-permute-done((bf16[2,16,5120]{2,1,0:T(8,128)(2,1)S(1)}, bf16[2,16,5120]{2,1,0:T(8,128)(2,1)S(1)}, u32[]{:S(2)}, u32[]{:S(2)}) %collective-permute-start.33) | collective-permute-done | bytes 327712 | tf_op jit(solution)/shard_map/cond/branch_22_fun/ppermute | solution.py:162
  50.7 1.3 %collective-permute-done.34 = bf16[2,16,5120]{2,1,0:T(8,128)(2,1)S(1)} collective-permute-done((bf16[2,16,5120]{2,1,0:T(8,128)(2,1)S(1)}, bf16[2,16,5120]{2,1,0:T(8,128)(2,1)S(1)}, u32[]{:S(2)}, u32[]{:S(2)}) %collective-permute-start.34) | collective-permute-done | bytes 327712 | tf_op jit(solution)/shard_map/cond/branch_22_fun/ppermute | solution.py:162
  52.1 0.0 copy-done.9
  52.1 4.8 %collective-permute-start.60 = (bf16[64,256]{1,0:T(8,128)(2,1)S(1)}, bf16[64,256]{1,0:T(8,128)(2,1)S(1)}, u32[]{:S(2)}, u32[]{:S(2)}) collective-permute-start(bf16[64,256]{1,0:T(8,128)(2,1)S(1)} %copy-done.9), channel_id=1, source_target_pairs={{0,1},{1,0},{2,3},{3,2},{4,5},{5,4},{6,7},{7,6},{8,9},{9,8},{10,11... | collective-permute-start | bytes 98312 | tf_op jit(solution)/shard_map/ppermute | solution.py:38
  56.9 0.0 copy-done.8
  56.9 0.2 collective-permute-start.61
  57.1 0.0 collective-permute-done.56.rest_0_
  57.1 0.0 copy-done.7
  57.1 2.3 %collective-permute-start.62 = (bf16[64,256]{1,0:T(8,128)(2,1)S(1)}, bf16[64,256]{1,0:T(8,128)(2,1)S(1)}, u32[]{:S(2)}, u32[]{:S(2)}) collective-permute-start(bf16[64,256]{1,0:T(8,128)(2,1)S(1)} %copy-done.7), channel_id=1, source_target_pairs={{0,3},{1,2},{2,1},{3,0},{4,7},{5,6},{6,5},{7,4},{8,11},{9,10},{10,... | collective-permute-start | bytes 98312 | tf_op jit(solution)/shard_map/ppermute | solution.py:38
  59.3 0.0 collective-permute-done.57.rest_1_
  59.3 0.0 collective-permute-done.60.rest_6_
  59.3 2.4 %collective-permute-done.61.rest_7_ = bf16[64,256]{1,0:T(8,128)(2,1)S(1)} collective-permute-done((bf16[64,256]{1,0:T(8,128)(2,1)S(1)}, bf16[64,256]{1,0:T(8,128)(2,1)S(1)}, u32[]{:S(2)}, u32[]{:S(2)}) %collective-permute-start.61) | collective-permute-done | bytes 32800 | tf_op jit(solution)/shard_map/ppermute | solution.py:38
  61.7 1.1 %collective-permute-done.62.rest_8_ = bf16[64,256]{1,0:T(8,128)(2,1)S(1)} collective-permute-done((bf16[64,256]{1,0:T(8,128)(2,1)S(1)}, bf16[64,256]{1,0:T(8,128)(2,1)S(1)}, u32[]{:S(2)}, u32[]{:S(2)}) %collective-permute-start.62) | collective-permute-done | bytes 32800 | tf_op jit(solution)/shard_map/ppermute | solution.py:38
  62.8 0.0 collective-permute-done.58.rest_2_
  62.8 0.0 copy-done
  62.8 0.0 copy-done.3
  62.8 0.0 copy-done.4
  62.8 0.0 copy-start.1
  62.8 0.0 copy-start.2
  62.8 3.2 %correlate.1 = (f32[128,128]{1,0:T(8,128)S(1)}, bf16[64,512]{1,0:T(8,128)(2,1)S(1)}) custom-call(s32[1]{0:T(128)} %bitcast.me_ref, s32[4,8]{1,0:T(4,128)S(1)} %copy-done.4, bf16[16,16,5120]{2,1,0:T(8,128)(2,1)} %fine_hbm.1, bf16[8,16,5120]{2,1,0:T(8,128)(2,1)S(1)} %copy-done, bf16[2,16,5120]{2,1,0:T(8,128)(2,1)S(1)} %collective-permute-done.56.rest_0_, ...), custom_call_target="tpu_custom_call" | custom-call | tf_op jit(solution)/shard_map/correlate/pallas_call | solution.py:356
  66.0 9.9 %all-gather = f32[1024,128]{1,0:T(8,128)S(1)} all-gather(f32[128,128]{1,0:T(8,128)S(1)} %get-tuple-element.248), channel_id=2, replica_groups=mesh['ga'=8,'ka'=4] {'ga'}, dimensions={0}, use_global_device_ids=true | all-gather | bytes 589824 | tf_op jit(solution)/shard_map/all_gather | solution.py:481
  75.8 0.0 copy-done.1
  75.8 0.0 copy-done.2
  75.9 1.7 %finish.1 = bf16[16,4096]{1,0:T(8,128)(2,1)} custom-call(f32[8,128,128]{2,1,0:T(8,128)S(1)} %bitcast.6, f32[128,128]{1,0:T(8,128)S(1)} %copy-done.2, bf16[128,1024]{1,0:T(8,128)(2,1)S(1)} %copy-done.1, bf16[64,512]{1,0:T(8,128)(2,1)S(1)} %get-tuple-element.250.left), custom_call_target="tpu_custom_call" | custom-call | tf_op jit(solution)/shard_map/finish/pallas_call | solution.py:422
  (2 shorter events, 0.0 us)
Async XLA Ops:
  0.0 9.7 %copy-start.5 = (bf16[6,64,512]{2,1,0:T(8,128)(2,1)S(1)}, bf16[6,64,512]{2,1,0:T(8,128)(2,1)}, u32[]{:S(2)}) copy-start(bf16[6,64,512]{2,1,0:T(8,128)(2,1)} %own_ref.1) | copy-start | bytes 1179652
  6.4 56.4 %collective-permute-start.58 = (bf16[4,16,5120]{2,1,0:T(8,128)(2,1)}, bf16[4,16,5120]{2,1,0:T(8,128)(2,1)S(1)}, u32[]{:S(2)}, u32[]{:S(2)}) collective-permute-start(bf16[4,16,5120]{2,1,0:T(8,128)(2,1)} %get-tuple-element.232), channel_id=1, source_target_pairs={{0,1},{1,0},{2,3},{3,2},{4,5},{5,4},{6,7},{7,6},{8,9},{9,8},{10,11... | collective-permute-start | bytes 1966088 | tf_op jit(solution)/shard_map/ppermute | solution.py:38
  9.7 6.9 %collective-permute-start.59 = (bf16[6,64,512]{2,1,0:T(8,128)(2,1)S(1)}, bf16[6,64,512]{2,1,0:T(8,128)(2,1)S(1)}, u32[]{:S(2)}, u32[]{:S(2)}) collective-permute-start(bf16[6,64,512]{2,1,0:T(8,128)(2,1)S(1)} %copy-done.5), channel_id=1, source_target_pairs={{0,28},{4,0},{8,4},{12,8},{16,12},{20,16},{24,20},{28,24},{1,29},{... | collective-permute-start | bytes 1179656 | tf_op jit(solution)/shard_map/ppermute | solution.py:33
  11.3 45.8 %collective-permute-start.56 = (bf16[2,16,5120]{2,1,0:T(8,128)(2,1)}, bf16[2,16,5120]{2,1,0:T(8,128)(2,1)S(1)}, u32[]{:S(2)}, u32[]{:S(2)}) collective-permute-start(bf16[2,16,5120]{2,1,0:T(8,128)(2,1)} %get-tuple-element.229), channel_id=1, source_target_pairs={{0,2},{1,3},{2,0},{3,1},{4,6},{5,7},{6,4},{7,5},{8,10},{9,11},{10,... | collective-permute-start | bytes 983048 | tf_op jit(solution)/shard_map/ppermute | solution.py:38
  14.0 45.3 %collective-permute-start.57 = (bf16[2,16,5120]{2,1,0:T(8,128)(2,1)}, bf16[2,16,5120]{2,1,0:T(8,128)(2,1)S(1)}, u32[]{:S(2)}, u32[]{:S(2)}) collective-permute-start(bf16[2,16,5120]{2,1,0:T(8,128)(2,1)} %get-tuple-element.230), channel_id=1, source_target_pairs={{0,3},{1,2},{2,1},{3,0},{4,7},{5,6},{6,5},{7,4},{8,11},{9,10},{10,... | collective-permute-start | bytes 983048 | tf_op jit(solution)/shard_map/ppermute | solution.py:38
  16.6 0.8 copy-start.6
  21.1 30.9 %copy-start.9 = (bf16[64,256]{1,0:T(8,128)(2,1)S(1)}, bf16[64,256]{1,0:T(8,128)(2,1)}, u32[]{:S(2)}) copy-start(bf16[64,256]{1,0:T(8,128)(2,1)} %get-tuple-element.245) | copy-start | bytes 98308
  21.2 35.7 %copy-start.8 = (bf16[64,256]{1,0:T(8,128)(2,1)S(1)}, bf16[64,256]{1,0:T(8,128)(2,1)}, u32[]{:S(2)}) copy-start(bf16[64,256]{1,0:T(8,128)(2,1)} %get-tuple-element.246) | copy-start | bytes 98308
  21.2 35.9 %copy-start.7 = (bf16[64,256]{1,0:T(8,128)(2,1)S(1)}, bf16[64,256]{1,0:T(8,128)(2,1)}, u32[]{:S(2)}) copy-start(bf16[64,256]{1,0:T(8,128)(2,1)} %get-tuple-element.247) | copy-start | bytes 98308
  21.2 41.6 %copy-start = (bf16[8,16,5120]{2,1,0:T(8,128)(2,1)S(1)}, bf16[8,16,5120]{2,1,0:T(8,128)(2,1)}, u32[]{:S(2)}) copy-start(bf16[8,16,5120]{2,1,0:T(8,128)(2,1)} %own_ref.2) | copy-start | bytes 3932164
  21.2 41.6 %copy-start.3 = (bf16[64,256]{1,0:T(8,128)(2,1)S(1)}, bf16[64,256]{1,0:T(8,128)(2,1)}, u32[]{:S(2)}) copy-start(bf16[64,256]{1,0:T(8,128)(2,1)} %get-tuple-element.244.rest_5_) | copy-start | bytes 98308
  21.2 41.6 %copy-start.4 = (s32[4,8]{1,0:T(4,128)S(1)}, s32[4,8]{1,0:T(4,128)}, u32[]{:S(2)}) copy-start(s32[4,8]{1,0:T(4,128)} %list_ref.6) | copy-start | bytes 388
  21.3 29.4 %collective-permute-start.33 = (bf16[2,16,5120]{2,1,0:T(8,128)(2,1)S(1)}, bf16[2,16,5120]{2,1,0:T(8,128)(2,1)S(1)}, u32[]{:S(2)}, u32[]{:S(2)}) collective-permute-start(bf16[2,16,5120]{2,1,0:T(8,128)(2,1)S(1)} %get-tuple-element.183), channel_id=1, source_target_pairs={{2,0},{0,2},{6,4},{4,6},{10,8},{8,10},{14,12},{12,14},{18,16},{16,... | collective-permute-start | bytes 983048 | tf_op jit(solution)/shard_map/cond/branch_22_fun/ppermute | solution.py:162
  26.1 26.0 %collective-permute-start.34 = (bf16[2,16,5120]{2,1,0:T(8,128)(2,1)S(1)}, bf16[2,16,5120]{2,1,0:T(8,128)(2,1)S(1)}, u32[]{:S(2)}, u32[]{:S(2)}) collective-permute-start(bf16[2,16,5120]{2,1,0:T(8,128)(2,1)S(1)} %get-tuple-element.184), channel_id=1, source_target_pairs={{2,1},{0,3},{6,5},{4,7},{10,9},{8,11},{14,13},{12,15},{18,17},{16,... | collective-permute-start | bytes 983048 | tf_op jit(solution)/shard_map/cond/branch_22_fun/ppermute | solution.py:162
  52.1 7.2 %collective-permute-start.60 = (bf16[64,256]{1,0:T(8,128)(2,1)S(1)}, bf16[64,256]{1,0:T(8,128)(2,1)S(1)}, u32[]{:S(2)}, u32[]{:S(2)}) collective-permute-start(bf16[64,256]{1,0:T(8,128)(2,1)S(1)} %copy-done.9), channel_id=1, source_target_pairs={{0,1},{1,0},{2,3},{3,2},{4,5},{5,4},{6,7},{7,6},{8,9},{9,8},{10,11... | collective-permute-start | bytes 98312 | tf_op jit(solution)/shard_map/ppermute | solution.py:38
  56.9 4.8 %collective-permute-start.61 = (bf16[64,256]{1,0:T(8,128)(2,1)S(1)}, bf16[64,256]{1,0:T(8,128)(2,1)S(1)}, u32[]{:S(2)}, u32[]{:S(2)}) collective-permute-start(bf16[64,256]{1,0:T(8,128)(2,1)S(1)} %copy-done.8), channel_id=1, source_target_pairs={{0,2},{1,3},{2,0},{3,1},{4,6},{5,7},{6,4},{7,5},{8,10},{9,11},{10,... | collective-permute-start | bytes 98312 | tf_op jit(solution)/shard_map/ppermute | solution.py:38
  57.1 5.7 %collective-permute-start.62 = (bf16[64,256]{1,0:T(8,128)(2,1)S(1)}, bf16[64,256]{1,0:T(8,128)(2,1)S(1)}, u32[]{:S(2)}, u32[]{:S(2)}) collective-permute-start(bf16[64,256]{1,0:T(8,128)(2,1)S(1)} %copy-done.7), channel_id=1, source_target_pairs={{0,3},{1,2},{2,1},{3,0},{4,7},{5,6},{6,5},{7,4},{8,11},{9,10},{10,... | collective-permute-start | bytes 98312 | tf_op jit(solution)/shard_map/ppermute | solution.py:38
  62.8 13.1 %copy-start.1 = (bf16[128,1024]{1,0:T(8,128)(2,1)S(1)}, bf16[128,1024]{1,0:T(8,128)(2,1)}, u32[]{:S(2)}) copy-start(bf16[128,1024]{1,0:T(8,128)(2,1)} %constant.10.clone.spread_ref) | copy-start | bytes 786436
  62.8 13.0 %copy-start.2 = (f32[128,128]{1,0:T(8,128)S(1)}, f32[128,128]{1,0:T(8,128)}, u32[]{:S(2)}) copy-start(f32[128,128]{1,0:T(8,128)} %get-tuple-element.249.scale_ref) | copy-start | bytes 196612
